TPU v7x, 32 devices: a whole 2x2x4 slice. The times are simulated.
32 devices in a mesh: tm: 8 (over z, y), coef: 4 (over x, core).
Axes of the slice: x: 2, y: 2, z: 4, core: 2. Of those that a mesh axis runs over, the one named last changes fastest.
Arguments:
- design: bfloat16 [2048, 50176], P('tm', 'coef'), may hold values from -0.0390625 to 0.0390625
- observed: float32 [2048, 128], P('tm'), may hold values from -6 to 6
- slab_counts: int32 [8], P('tm'), may hold values from 128 to 256, as said below
- gap_mask: int32 [2048], P('tm'), may hold values 0 or 1
- filter_taps: float32 [128], replicated, may hold values from -0.5 to 1.2, as said below
- kaula_diag: float32 [50176], P('coef'), may hold values from 0.1 to 1
- precond: float32 [50176], P('coef'), may hold values from 0.3 to 3
Outputs:
- solution: float32 [50176, 128], P(('coef', 'tm'))
- residual: float32 [50176, 128], P(('coef', 'tm'))
Inputs may be any that keep to these rules, and one draw needn't show every extreme that they name: `slab_counts`: every slab holds at most 256 valid epochs, and some slab holds exactly 256. filter_taps[0] lies between 1 and 1.2.
All inputs are finite; a program needn't handle non-finite values. No bound on the sum of `gap_mask` on one device may be relied on, other than what follows from the above.
Results may differ from a plain program's by a relative error of at most 0.0065.
The roundings to bfloat16 on the way count: a program that leaves them out, or rounds other values in their place, can miss the bound.
Values may be sent and summed in bfloat16 or wider, within the bound.
A program may use at most 64 MiB of HBM per device.

v0:
```python
import jax
import jax.numpy as jnp
from jax import lax
from jax.sharding import PartitionSpec as P

ITERS = 2
HIGHEST = lax.Precision.HIGHEST


def toeplitz(pattern, band_len):
    tiled = jnp.tile(pattern, band_len)[: band_len * (2 * band_len - 1)]
    return tiled.reshape(band_len, 2 * band_len - 1)[:, :band_len]


def block_pair(filter_taps):
    band_len = filter_taps.shape[0]
    spacer = jnp.zeros((band_len,), jnp.float32)
    reversed_taps = filter_taps[:0:-1]
    lower = jnp.concatenate([filter_taps[:1], spacer, reversed_taps])
    upper = jnp.concatenate([jnp.zeros((1,), jnp.float32), reversed_taps, spacer])
    return (toeplitz(lower, band_len), toeplitz(upper, band_len))


def forward(values, lower_block, upper_block):
    band_len = lower_block.shape[0]
    blocks = values.reshape(-1, band_len, values.shape[1])
    previous = jnp.concatenate([jnp.zeros_like(blocks[:1]), blocks[:-1]], 0)
    result = jnp.einsum("ij,bjr->bir", lower_block, blocks, precision=HIGHEST)
    result = result + jnp.einsum("ij,bjr->bir", upper_block, previous, precision=HIGHEST)
    return result.reshape(values.shape)


def backward(values, lower_block, upper_block):
    band_len = lower_block.shape[0]
    blocks = values.reshape(-1, band_len, values.shape[1])
    following = jnp.concatenate([blocks[1:], jnp.zeros_like(blocks[:1])], 0)
    result = jnp.einsum("ji,bjr->bir", lower_block, blocks, precision=HIGHEST)
    result = result + jnp.einsum("ji,bjr->bir", upper_block, following, precision=HIGHEST)
    return result.reshape(values.shape)


def shards(design, observed, slab_counts, gap_mask, filter_taps, kaula_diag, precond):
    epoch_rows, coef_rows = design.shape
    columns = observed.shape[1]
    slabs = lax.axis_size("tm")
    epochs = slabs * epoch_rows
    owned_rows = coef_rows // slabs
    owner_index = lax.axis_index("tm")
    lower_block, upper_block = block_pair(filter_taps)
    position = jnp.arange(epoch_rows, dtype=jnp.int32)
    local_weight = ((gap_mask == 1) & (position < slab_counts[0])).astype(jnp.float32)
    packed = jnp.concatenate([observed, local_weight.reshape(-1, columns)], 0)
    gathered = lax.all_gather(packed, "tm", axis=0, tiled=False)
    all_observed = gathered[:, :epoch_rows].reshape(epochs, columns)
    weight = gathered[:, epoch_rows:].reshape(epochs, 1)
    block = lax.all_to_all(design, "tm", split_axis=1, concat_axis=0, tiled=True)

    def weighted(values):
        inner = forward(weight * values, lower_block, upper_block)
        return (weight * backward(inner, lower_block, upper_block)).astype(jnp.bfloat16)

    def transposed(filtered):
        return lax.dot_general(
            block, filtered, (((0,), (0,)), ((), ())), preferred_element_type=jnp.float32
        )

    def summed(scaled, terms):
        partial = jnp.dot(block, scaled.astype(jnp.bfloat16), preferred_element_type=jnp.float32)
        rows = [jnp.sum(term, 0)[None] for term in terms]
        rows.append(jnp.zeros((8 - len(rows), columns), jnp.float32))
        total = lax.psum(jnp.concatenate([partial] + rows, 0), ("tm", "coef"))
        return (total[:epochs], [total[epochs + at] for at in range(len(terms))])

    start = owner_index * owned_rows
    kaula_col = lax.dynamic_slice_in_dim(kaula_diag, start, owned_rows, 0)[:, None]
    precond_col = lax.dynamic_slice_in_dim(precond, start, owned_rows, 0)[:, None]
    residual = transposed(weighted(all_observed))
    solution = jnp.zeros_like(residual)
    for iteration in range(ITERS):
        scaled = precond_col * residual
        terms = [residual * scaled, kaula_col * scaled * scaled]
        if iteration == 0:
            slab_values, (norm_now, ridge) = summed(scaled, terms)
            direction = scaled
        else:
            terms.append(kaula_col * scaled * direction)
            fresh, (norm_next, own_ridge, cross) = summed(scaled, terms)
            ratio = norm_next / norm_now
            slab_values = fresh + ratio * slab_values
            ridge = own_ridge + ratio * (2.0 * cross + ratio * ridge)
            direction = scaled + ratio * direction
            norm_now = norm_next
        filtered = weighted(slab_values)
        curvature = ridge + jnp.sum(slab_values * filtered.astype(jnp.float32), 0)
        step_len = norm_now / curvature
        image = transposed(filtered) + kaula_col * direction
        solution = solution + step_len * direction
        residual = residual - step_len * image
    return (solution, residual)


def solution(mesh):
    placed = (P("tm", "coef"), P("tm", None), P("tm"), P("tm"), P(), P("coef"), P("coef"))
    return jax.shard_map(
        shards,
        mesh=mesh,
        in_specs=placed,
        out_specs=(P(("coef", "tm"), None), P(("coef", "tm"), None)),
        check_vma=False,
    )
```

profile of v0, /device:TPU:0, one launch (start us, length us, event | category | flops | bytes accessed | tf_op | source)
XLA Modules:
  0.0 508.5 jit_solution(15422720378014263486)
XLA Ops:
  7.2 9.5 %copy.77 = bf16[256,12544]{0,1:T(8,128)(2,1)} copy(bf16[256,12544]{1,0:T(8,128)(2,1)} %param.7) | data formatting | bytes 12845056 | tf_op args[0]
  16.7 7.4 %all-to-all-start = ((bf16[256,8,1568]{0,2,1:T(8,128)(2,1)}), bf16[256,8,1568]{0,2,1:T(8,128)(2,1)}, u32[]{:S(2)}, u32[]{:S(2)}) async-start(bf16[256,8,1568]{0,2,1:T(8,128)(2,1)} %bitcast.147), calls=%async_computation | async-start | bytes 12845056 | tf_op jit(solution)/shard_map/all_to_all | solution.py:56
  28.3 150.4 %all-gather.4.cloned.1.call-done = f32[8,258,128]{2,1,0:T(8,128)} async-done(((f32[1,258,128]{2,1,0:T(8,128)}), f32[8,258,128]{2,1,0:T(8,128)}) %all-gather.4.cloned.1.call-update) | async-done | bytes 1056784 | tf_op jit(solution)/shard_map/all_gather | solution.py:53
  181.6 2.1 fusion.19
  183.8 1.7 fusion.8
  187.7 3.7 copy.127
  191.4 1.9 fusion.27
  197.1 128.1 %all-reduce.9.cloned.1.call-done = f32[2056,128]{0,1:T(8,128)} async-done(((f32[2056,128]{0,1:T(8,128)}), f32[2056,128]{0,1:T(8,128)}) %all-reduce.9.cloned.1.call-update) | async-done | bytes 1052688 | tf_op jit(solution)/shard_map/psum | solution.py:71
  325.2 1.4 slice_multiply_fusion
  328.1 1.7 fusion.7
  330.9 2.0 fusion.18
  332.8 1.3 copy.120
  334.2 2.1 multiply_reduce_fusion.1
  337.3 5.3 %fusion.29 = (f32[128]{0:T(128)S(1)}, f32[128]{0:T(128)S(1)}, f32[128]{0:T(128)S(1)}, f32[1568,128]{1,0:T(8,128)S(1)}) fusion(f32[1568,128]{1,0:T(8,128)} %copy-done.2, f32[1568]{0:T(1024)} %copy-done.10, f32[1568]{0:T(1024)S(1)} %dynamic_slice.6, bf16[2048,1568]{0,1:T(8,128)(2,1)} %bitcast.142, bf16[2048,128]{1,0:T(8,128)(2,1)} %bitcast.166, ...), kind=kOutput, calls=%fused_computation.58 | convolution fusion | flops 824692352 | bytes 8567040 | tf_op jit(solution)/shard_map/dot_general | solution.py:63
  342.6 2.2 convolution_bitcast_fusion.3
  345.2 2.4 concatenate.41
  347.7 130.8 %all-reduce.11.cloned.1.call-done = f32[2056,128]{0,1:T(8,128)} async-done(((f32[2056,128]{0,1:T(8,128)}), f32[2056,128]{0,1:T(8,128)}) %all-reduce.11.cloned.1.call-update) | async-done | bytes 1052688 | tf_op jit(solution)/shard_map/psum | solution.py:71
  479.4 1.4 broadcast_multiply_fusion
  482.9 1.5 copy.94
  484.4 1.7 fusion.6
  487.3 2.2 fusion.17
  489.5 2.6 copy.123
  492.1 1.8 multiply_reduce_fusion
  496.4 5.5 %fusion.5 = f32[1568,128]{1,0:T(8,128)} fusion(f32[1568,128]{1,0:T(8,128)S(1)} %copy-done.5, bf16[2048,1568]{0,1:T(8,128)(2,1)} %bitcast.143, bf16[2048,128]{1,0:T(8,128)(2,1)S(1)} %bitcast.155, f32[1568,128]{1,0:T(8,128)S(1)} %copy-done.3, f32[128]{0:T(128)S(1)} %fusion.44, f32[128]{0:T(128)S(1)} %fusion.39, f32[1568]{0:T(1024)S(1)} %copy-done.11, ...), kind=kOutput, calls=%fused_computation.10 | convolution fusion | flops 823689216 | bytes 9368832 | tf_op jit(solution)/shard_map/dot_general | solution.py:63
  (87 shorter events, 22.6 us)
Async XLA Ops:
  16.7 8.1 %copy-start.14 = (s32[256]{0:T(256)S(1)}, s32[256]{0:T(256)}, u32[]{:S(2)}) copy-start(s32[256]{0:T(256)} %param.10) | copy-start | bytes 3076
  16.7 8.2 %copy-start.9 = (f32[256,128]{1,0:T(8,128)S(1)}, f32[256,128]{1,0:T(8,128)}, u32[]{:S(2)}) copy-start(f32[256,128]{1,0:T(8,128)} %param.8) | copy-start | bytes 393220
  16.7 10.5 %copy-start.15 = (f32[128]{0:T(128)S(1)}, f32[128]{0:T(128)}, u32[]{:S(2)}) copy-start(f32[128]{0:T(128)} %param.11) | copy-start | bytes 1540
  16.7 171.0 %all-to-all-start = ((bf16[256,8,1568]{0,2,1:T(8,128)(2,1)}), bf16[256,8,1568]{0,2,1:T(8,128)(2,1)}, u32[]{:S(2)}, u32[]{:S(2)}) async-start(bf16[256,8,1568]{0,2,1:T(8,128)(2,1)} %bitcast.147), calls=%async_computation | async-start | bytes 12845056 | tf_op jit(solution)/shard_map/all_to_all | solution.py:56
  24.1 154.6 %all-gather.4.cloned.1.call-start = ((), (), s32[]{:S(2)}) async-start(), calls=%async_computation.3 | async-start | bytes 1216512 | tf_op jit(solution)/shard_map/all_gather | solution.py:53
  25.6 299.7 %all-reduce.9.cloned.1.call-start = ((), (), s32[]{:S(2)}) async-start(), calls=%async_computation.1 | async-start | bytes 2228224 | tf_op jit(solution)/shard_map/psum | solution.py:71
  26.4 165.0 %copy-start.10 = (f32[1568]{0:T(1024)}, f32[1568]{0:T(1024)S(1)}, u32[]{:S(2)}) copy-start(f32[1568]{0:T(1024)S(1)} %dynamic_slice.7) | copy-start | bytes 18820
  27.9 157.6 %copy-start.6 = (f32[128,255]{1,0:T(8,128)}, f32[128,255]{1,0:T(8,128)S(1)}, u32[]{:S(2)}) copy-start(f32[128,255]{1,0:T(8,128)S(1)} %reshape.76) | copy-start | bytes 391684
  191.4 2.7 copy-start
  193.4 2.0 copy-start.2
  195.4 131.7 %copy-start.7 = (f32[128,255]{1,0:T(8,128)S(1)}, f32[128,255]{1,0:T(8,128)}, u32[]{:S(2)}) copy-start(f32[128,255]{1,0:T(8,128)} %copy-done.6) | copy-start | bytes 391684
  196.9 281.6 %all-reduce.11.cloned.1.call-start = ((), (), s32[]{:S(2)}) async-start(), calls=%async_computation.2 | async-start | bytes 2228224 | tf_op jit(solution)/shard_map/psum | solution.py:71
  325.2 1.8 copy-start.1
  334.2 8.5 %slice-start = ((s8[6422528]{0:T(1024)(128)(4,1)}), s8[2228224]{0:T(1024)(128)(4,1)S(1)}, s32[]{:S(2)}) async-start(s8[6422528]{0:T(1024)(128)(4,1)} %bitcast.144), calls=%async_computation.4 | async-start | bytes 4456448
  337.3 5.3 %copy-start.12 = (f32[128]{0:T(128)}, f32[128]{0:T(128)S(1)}, u32[]{:S(2)}) copy-start(f32[128]{0:T(128)S(1)} %fusion.38) | copy-start | bytes 1540
  337.3 5.4 %slice-start.1 = ((s8[6422528]{0:T(1024)(128)(4,1)}), s8[4194304]{0:T(1024)(128)(4,1)S(1)}, s32[]{:S(2)}) async-start(s8[6422528]{0:T(1024)(128)(4,1)} %bitcast.144), calls=%async_computation.5 | async-start | bytes 8388608
  342.6 2.3 copy-start.4
  344.9 135.9 %copy-start.8 = (f32[128,255]{1,0:T(8,128)S(1)}, f32[128,255]{1,0:T(8,128)}, u32[]{:S(2)}) copy-start(f32[128,255]{1,0:T(8,128)} %copy-done.6) | copy-start | bytes 391684
  486.2 9.1 %copy-start.3 = (f32[1568,128]{1,0:T(8,128)S(1)}, f32[1568,128]{1,0:T(8,128)}, u32[]{:S(2)}) copy-start(f32[1568,128]{1,0:T(8,128)} %copy-done.2) | copy-start | bytes 2408452
  486.2 9.1 %copy-start.5 = (f32[1568,128]{1,0:T(8,128)S(1)}, f32[1568,128]{1,0:T(8,128)}, u32[]{:S(2)}) copy-start(f32[1568,128]{1,0:T(8,128)} %copy-done.4) | copy-start | bytes 2408452
  486.2 9.1 %copy-start.13 = (f32[128]{0:T(128)S(1)}, f32[128]{0:T(128)}, u32[]{:S(2)}) copy-start(f32[128]{0:T(128)} %copy-done.12) | copy-start | bytes 1540
  487.3 9.1 %copy-start.11 = (f32[1568]{0:T(1024)S(1)}, f32[1568]{0:T(1024)}, u32[]{:S(2)}) copy-start(f32[1568]{0:T(1024)} %copy-done.10) | copy-start | bytes 18820
Sparse Core Ops, SparseCore 0:
  27.7 151.0 all-gather.3
  197.0 128.1 all-reduce.8
  347.8 130.6 all-reduce.10
where the time goes:
time: 510 us; the launch traced here: 509 us
  waiting for transfers between devices  409 us (80%)
  matrix products  33.9 us (7%)
  local copies, waits for them, and re-layouts  31.5 us (6%)
  between operations  14.8 us (3%)
  other arithmetic  11.1 us (2%)
  starting transfers between devices  7.75 us (2%)
    psum x2, waiting for transfers between devices, summed(): total = lax.psum(jnp.concatenate([partial] + rows, 0), ('tm', 'coef'))  259 us
    all_gather x1, waiting for transfers between devices, shards(): gathered = lax.all_gather(packed, 'tm', axis=0, tiled=False)  150 us
    dot_general x3, matrix products, transposed(): lax.dot_general(block, filtered, (((0,), (0,)), ((), ())), preferred_elem...  12.8 us
    unnamed x41, local copies, waits for them, and re-layouts  10.8 us
  transfers between devices with their start and end apart: 4, of which 3 were waited for; matrix products, arithmetic and copies ran while one was open for 2% of the time, Pallas kernels for 0%

commit v1 on v0

--- a/solution.py
+++ b/solution.py
@@ -68,7 +68,8 @@
         partial = jnp.dot(block, scaled.astype(jnp.bfloat16), preferred_element_type=jnp.float32)
         rows = [jnp.sum(term, 0)[None] for term in terms]
         rows.append(jnp.zeros((8 - len(rows), columns), jnp.float32))
-        total = lax.psum(jnp.concatenate([partial] + rows, 0), ("tm", "coef"))
+        partial_2 = lax.psum(jnp.concatenate([partial] + rows, 0), "coef")
+        total = lax.psum(partial_2, "tm")
         return (total[:epochs], [total[epochs + at] for at in range(len(terms))])
 
     start = owner_index * owned_rows

time: 510 us -> 485 us (0.951)
  waiting for transfers between devices: 409 us -> 387 us
    psum x2 -> x4, waiting for transfers between devices: 259 us -> 236 us  [the longest x2 166 us: summed(): total = lax.psum(partial_2, 'tm')]
  transfers between devices with their start and end apart: 4 -> 6, of which waited for: 3 -> 5; matrix products, arithmetic and copies ran while one was open for 2% -> 3% of each run, Pallas kernels for 0% -> 0%
where the time goes in v1:
time: 485 us; the launch traced here: 484 us
  waiting for transfers between devices  387 us (80%)
  matrix products  33 us (7%)
  local copies, waits for them, and re-layouts  30.8 us (6%)
  between operations  14.8 us (3%)
  other arithmetic  11.2 us (2%)
  starting transfers between devices  8.05 us (2%)
    psum x2, waiting for transfers between devices, summed(): total = lax.psum(partial_2, 'tm')  166 us
    all_gather x1, waiting for transfers between devices, shards(): gathered = lax.all_gather(packed, 'tm', axis=0, tiled=False)  150 us
    psum x2, waiting for transfers between devices, summed(): partial_2 = lax.psum(jnp.concatenate([partial] + rows, 0), 'coef')  70.2 us
    dot_general x3, matrix products, transposed(): lax.dot_general(block, filtered, (((0,), (0,)), ((), ())), preferred_elem...  12.8 us
    unnamed x41, local copies, waits for them, and re-layouts  11.7 us
  transfers between devices with their start and end apart: 6, of which 5 were waited for; matrix products, arithmetic and copies ran while one was open for 3% of the time, Pallas kernels for 0%

profile of v1, /device:TPU:0, one launch (start us, length us, event | category | flops | bytes accessed | tf_op | source)
XLA Modules:
  0.0 484.4 jit_solution(15101037773644732059)
XLA Ops:
  7.2 9.5 %copy.77 = bf16[256,12544]{0,1:T(8,128)(2,1)} copy(bf16[256,12544]{1,0:T(8,128)(2,1)} %param.7) | data formatting | bytes 12845056 | tf_op args[0]
  16.7 7.4 %all-to-all-start = ((bf16[256,8,1568]{0,2,1:T(8,128)(2,1)}), bf16[256,8,1568]{0,2,1:T(8,128)(2,1)}, u32[]{:S(2)}, u32[]{:S(2)}) async-start(bf16[256,8,1568]{0,2,1:T(8,128)(2,1)} %bitcast.147), calls=%async_computation | async-start | bytes 12845056 | tf_op jit(solution)/shard_map/all_to_all | solution.py:56
  28.3 150.4 %all-gather.4.cloned.1.call-done = f32[8,258,128]{2,1,0:T(8,128)} async-done(((f32[1,258,128]{2,1,0:T(8,128)}), f32[8,258,128]{2,1,0:T(8,128)}) %all-gather.4.cloned.1.call-update) | async-done | bytes 1056784 | tf_op jit(solution)/shard_map/all_gather | solution.py:53
  181.6 2.1 fusion.19
  183.8 1.7 fusion.8
  187.7 3.7 copy.127
  191.4 1.9 fusion.27
  196.9 34.3 %all-reduce.11.cloned.1.call-done = f32[2056,128]{0,1:T(8,128)} async-done(((f32[2056,128]{0,1:T(8,128)}), f32[2056,128]{0,1:T(8,128)}) %all-reduce.11.cloned.1.call-update) | async-done | bytes 1052688 | tf_op jit(solution)/shard_map/psum | solution.py:71
  231.5 82.9 %all-reduce.13.cloned.1.call-done = f32[2056,128]{0,1:T(8,128)} async-done(((f32[2056,128]{0,1:T(8,128)}), f32[2056,128]{0,1:T(8,128)}) %all-reduce.13.cloned.1.call-update) | async-done | bytes 1052688 | tf_op jit(solution)/shard_map/psum | solution.py:72
  318.0 1.7 fusion.7
  320.8 1.9 fusion.18
  322.8 1.3 copy.120
  324.1 2.1 multiply_reduce_fusion.1
  327.2 5.3 %fusion.29 = (f32[128]{0:T(128)S(1)}, f32[128]{0:T(128)S(1)}, f32[128]{0:T(128)S(1)}, f32[1568,128]{1,0:T(8,128)S(1)}) fusion(f32[1568,128]{1,0:T(8,128)} %copy-done.2, f32[1568]{0:T(1024)} %copy-done.10, f32[1568]{0:T(1024)S(1)} %dynamic_slice.6, bf16[2048,1568]{0,1:T(8,128)(2,1)} %bitcast.142, bf16[2048,128]{1,0:T(8,128)(2,1)} %bitcast.166, ...), kind=kOutput, calls=%fused_computation.58 | convolution fusion | flops 824692352 | bytes 8567040 | tf_op jit(solution)/shard_map/dot_general | solution.py:63
  332.6 2.3 convolution_bitcast_fusion.3
  335.2 2.2 concatenate.41
  337.6 35.9 %all-reduce.15.cloned.1.call-done = f32[2056,128]{0,1:T(8,128)} async-done(((f32[2056,128]{0,1:T(8,128)}), f32[2056,128]{0,1:T(8,128)}) %all-reduce.15.cloned.1.call-update) | async-done | bytes 1052688 | tf_op jit(solution)/shard_map/psum | solution.py:71
  373.6 83.0 %all-reduce.17.cloned.1.call-done = f32[2056,128]{0,1:T(8,128)} async-done(((f32[2056,128]{0,1:T(8,128)}), f32[2056,128]{0,1:T(8,128)}) %all-reduce.17.cloned.1.call-update) | async-done | bytes 1052688 | tf_op jit(solution)/shard_map/psum | solution.py:72
  457.5 1.4 broadcast_multiply_fusion
  461.0 1.5 copy.94
  462.5 1.7 fusion.6
  466.5 1.3 copy.123
  467.8 2.0 multiply_reduce_fusion
  472.3 5.6 %fusion.5 = f32[1568,128]{1,0:T(8,128)} fusion(f32[1568,128]{1,0:T(8,128)S(1)} %copy-done.5, bf16[2048,1568]{0,1:T(8,128)(2,1)} %bitcast.143, bf16[2048,128]{1,0:T(8,128)(2,1)S(1)} %bitcast.155, f32[1568,128]{1,0:T(8,128)S(1)} %copy-done.3, f32[128]{0:T(128)S(1)} %fusion.44, f32[128]{0:T(128)S(1)} %fusion.39, f32[1568]{0:T(1024)S(1)} %copy-done.11, ...), kind=kOutput, calls=%fused_computation.10 | convolution fusion | flops 823689216 | bytes 9368832 | tf_op jit(solution)/shard_map/dot_general | solution.py:63
  (93 shorter events, 26.3 us)
Async XLA Ops:
  16.7 8.1 %copy-start.14 = (s32[256]{0:T(256)S(1)}, s32[256]{0:T(256)}, u32[]{:S(2)}) copy-start(s32[256]{0:T(256)} %param.10) | copy-start | bytes 3076
  16.7 8.2 %copy-start.9 = (f32[256,128]{1,0:T(8,128)S(1)}, f32[256,128]{1,0:T(8,128)}, u32[]{:S(2)}) copy-start(f32[256,128]{1,0:T(8,128)} %param.8) | copy-start | bytes 393220
  16.7 10.5 %copy-start.15 = (f32[128]{0:T(128)S(1)}, f32[128]{0:T(128)}, u32[]{:S(2)}) copy-start(f32[128]{0:T(128)} %param.11) | copy-start | bytes 1540
  16.7 171.0 %all-to-all-start = ((bf16[256,8,1568]{0,2,1:T(8,128)(2,1)}), bf16[256,8,1568]{0,2,1:T(8,128)(2,1)}, u32[]{:S(2)}, u32[]{:S(2)}) async-start(bf16[256,8,1568]{0,2,1:T(8,128)(2,1)} %bitcast.147), calls=%async_computation | async-start | bytes 12845056 | tf_op jit(solution)/shard_map/all_to_all | solution.py:56
  24.1 154.6 %all-gather.4.cloned.1.call-start = ((), (), s32[]{:S(2)}) async-start(), calls=%async_computation.5 | async-start | bytes 1216512 | tf_op jit(solution)/shard_map/all_gather | solution.py:53
  25.6 205.6 %all-reduce.11.cloned.1.call-start = ((), (), s32[]{:S(2)}) async-start(), calls=%async_computation.1 | async-start | bytes 2228224 | tf_op jit(solution)/shard_map/psum | solution.py:71
  26.4 165.0 %copy-start.10 = (f32[1568]{0:T(1024)}, f32[1568]{0:T(1024)S(1)}, u32[]{:S(2)}) copy-start(f32[1568]{0:T(1024)S(1)} %dynamic_slice.7) | copy-start | bytes 18820
  27.9 157.6 %copy-start.6 = (f32[128,255]{1,0:T(8,128)}, f32[128,255]{1,0:T(8,128)S(1)}, u32[]{:S(2)}) copy-start(f32[128,255]{1,0:T(8,128)S(1)} %reshape.76) | copy-start | bytes 391684
  191.4 2.7 copy-start
  193.4 2.0 copy-start.2
  196.9 117.4 %all-reduce.13.cloned.1.call-start = ((), (), s32[]{:S(2)}) async-start(), calls=%async_computation.2 | async-start | bytes 2228224 | tf_op jit(solution)/shard_map/psum | solution.py:72
  231.2 142.3 %all-reduce.15.cloned.1.call-start = ((), (), s32[]{:S(2)}) async-start(), calls=%async_computation.3 | async-start | bytes 2228224 | tf_op jit(solution)/shard_map/psum | solution.py:71
  315.7 1.2 copy-start.1
  315.8 1.2 copy-start.7
  324.1 8.5 %slice-start = ((s8[6422528]{0:T(1024)(128)(4,1)}), s8[2228224]{0:T(1024)(128)(4,1)S(1)}, s32[]{:S(2)}) async-start(s8[6422528]{0:T(1024)(128)(4,1)} %bitcast.144), calls=%async_computation.6 | async-start | bytes 4456448
  327.2 5.3 %copy-start.12 = (f32[128]{0:T(128)}, f32[128]{0:T(128)S(1)}, u32[]{:S(2)}) copy-start(f32[128]{0:T(128)S(1)} %fusion.38) | copy-start | bytes 1540
  327.2 5.4 %slice-start.1 = ((s8[6422528]{0:T(1024)(128)(4,1)}), s8[4194304]{0:T(1024)(128)(4,1)S(1)}, s32[]{:S(2)}) async-start(s8[6422528]{0:T(1024)(128)(4,1)} %bitcast.144), calls=%async_computation.7 | async-start | bytes 8388608
  332.5 2.3 copy-start.4
  337.4 119.1 %all-reduce.17.cloned.1.call-start = ((), (), s32[]{:S(2)}) async-start(), calls=%async_computation.4 | async-start | bytes 2228224 | tf_op jit(solution)/shard_map/psum | solution.py:72
  457.5 1.5 copy-start.8
  467.8 3.3 copy-start.3
  467.8 3.3 copy-start.5
  467.8 3.3 copy-start.13
  471.1 1.2 copy-start.11
Sparse Core Ops, SparseCore 0:
  27.7 151.0 all-gather.3
  197.0 34.1 all-reduce.10
  234.7 79.5 all-reduce.12
  337.5 35.9 all-reduce.14
  376.9 79.5 all-reduce.16
